TPU v7x, 256 devices: a whole 4x4x8 slice. The times are simulated.
256 devices in a mesh: dp: 32 (over z, x), mp: 8 (over y, core).
Axes of the slice: x: 4, y: 4, z: 8, core: 2. Of those that a mesh axis runs over, the one named last changes fastest.
Arguments:
- activations: bfloat16 [16384, 3072], P('dp', 'mp'), may hold values from -6 to 6
- out_grads: bfloat16 [16384, 6144], P('dp', 'mp'), may hold values from -0.25 to 0.25
- error: bfloat16 [32, 3072, 6144], P('dp', 'mp'), may hold values from -8 to 8
- sketch: bfloat16 [6144, 64], replicated, may hold values from -0.078125 to 0.078125
- momentum: float32 [3072, 6144], P('mp', 'dp'), may hold values from -6 to 6
Outputs:
- error_new: bfloat16 [32, 3072, 6144], P('dp', 'mp')
- momentum_new: float32 [3072, 6144], P('mp', 'dp')
- next_sketch: bfloat16 [6144, 64], replicated
All inputs are finite; a program needn't handle non-finite values.
Results may differ from a plain program's by a relative error of at most 0.0057.
Values may be sent and summed in bfloat16 or wider, within the bound.
No kernel may reach another device: no remote copies, remote signals or barrier semaphores. Data moves between devices by JAX's collectives and lax.ppermute only.
A program may use at most 64 MiB of HBM per device.

v0:
```python
import jax
import jax.numpy as jnp
from jax import lax
from jax.sharding import Mesh
from jax.sharding import PartitionSpec as P

MP = ("mp_0", "mp_1")
DP = ("dp_0", "dp_1")
beta_decay = 0.9


def cut_along(shard, dim, peers):
    before, after = (shard.shape[:dim], shard.shape[dim + 1 :])
    return jnp.moveaxis(shard.reshape(*before, peers, -1, *after), dim, 0)


def summed_on_arrival(shard, axis, dim):
    blocks = cut_along(shard, dim, lax.axis_size(axis))
    arrived = lax.all_to_all(blocks, axis, split_axis=0, concat_axis=0, tiled=True)
    return arrived.sum(axis=0)


def filled_up(lines, peers):
    spare = -lines.shape[0] % peers
    if not spare:
        return lines
    return jnp.concatenate([lines, jnp.zeros((spare, *lines.shape[1:]), lines.dtype)])


def in_order(blocks, dim):
    blocks = jnp.moveaxis(blocks, 0, dim)
    dims = blocks.shape
    return blocks.reshape(*dims[:dim], dims[dim] * dims[dim + 1], *dims[dim + 2 :])


def copy_for_each(shard, axis):
    copies = jnp.broadcast_to(shard, (lax.axis_size(axis), *shard.shape))
    return lax.all_to_all(copies, axis, split_axis=0, concat_axis=0, tiled=True)


def collect(shard, axis, dim):
    return in_order(copy_for_each(shard, axis), dim)


def nested_sum(shard, axes):
    lines = shard.reshape(-1, shard.shape[-1])
    own = summed_on_arrival(filled_up(lines, lax.axis_size(axes)), axes, 0)
    whole = collect(own, axes, 0)
    return whole[: len(lines)].reshape(shard.shape)


def over_copies(shard, axis):
    return copy_for_each(shard, axis).sum(axis=0)


def gathered_by_axis(shard, axes, dim):
    far, near = axes
    blocks = copy_for_each(copy_for_each(shard, far), near)
    return in_order(blocks.swapaxes(0, 1).reshape(-1, *shard.shape), dim)


def sum_in_two_steps(shard, axes, dim):
    far, near = axes
    own = summed_on_arrival(cut_along(shard, dim, lax.axis_size(far)), near, dim + 1)
    return jnp.sum(lax.all_to_all(own, far, 0, 0, tiled=True), axis=0)


def total_of(shard, axes):
    lines = shard.reshape(-1, shard.shape[-1])
    padded = filled_up(lines, lax.axis_size(axes[0]) * lax.axis_size(axes[1]))
    whole = gathered_by_axis(sum_in_two_steps(padded, axes, 0), axes, 0)
    return lax.slice_in_dim(whole, 0, len(lines)).reshape(shard.shape)


def update_momentum(momentum, basis_rows, sketch_block):
    product = lax.dot_general(
        basis_rows, sketch_block, (((1,), (1,)), ((), ())), preferred_element_type=jnp.float32
    )
    return beta_decay * momentum + product


def local(activations, out_grads, error, sketch, momentum):
    own_error = error[0]
    product = lax.dot_general(
        activations,
        lax.all_gather(out_grads, MP, axis=1, tiled=True),
        (((0,), (0,)), ((), ())),
        preferred_element_type=jnp.float32,
    )
    accumulated = (product + own_error.astype(jnp.float32)).astype(jnp.bfloat16)
    local_left = jnp.dot(accumulated, sketch, preferred_element_type=jnp.float32)
    left_sketch = nested_sum(local_left, DP)
    gram_local = jnp.dot(
        left_sketch.T,
        left_sketch,
        precision=lax.Precision.HIGHEST,
        preferred_element_type=jnp.float32,
    )
    gram_matrix = over_copies(gram_local, MP)
    factor = jnp.linalg.cholesky(gram_matrix)
    basis_rows = jax.scipy.linalg.solve_triangular(factor, left_sketch.T, lower=True).T.astype(
        jnp.bfloat16
    )
    block_width = momentum.shape[1]
    local_right = lax.dot_general(
        accumulated, basis_rows, (((0,), (0,)), ((), ())), preferred_element_type=jnp.float32
    )
    right_sketch = total_of(local_right, (("dp_0", "dp_1"), ("mp_0", "mp_1")))
    next_sketch = right_sketch.astype(jnp.bfloat16)
    sketch_part = lax.dynamic_slice_in_dim(
        next_sketch, lax.axis_index(DP) * block_width, block_width, 0
    )
    momentum_new = update_momentum(momentum, basis_rows, sketch_part)
    decoded = lax.dot_general(
        basis_rows, next_sketch, (((1,), (1,)), ((), ())), preferred_element_type=jnp.float32
    )
    error_new = (accumulated.astype(jnp.float32) - decoded / lax.axis_size(DP)).astype(jnp.bfloat16)
    return (error_new[None], momentum_new, next_sketch)


def solution(mesh):
    split = Mesh(mesh.devices.reshape(8, 4, 4, 2), ("dp_0", "dp_1", "mp_0", "mp_1"))
    placed = (P(DP, MP), P(DP, MP), P(DP, MP, None), P(), P(MP, DP))
    return jax.shard_map(
        local,
        mesh=split,
        in_specs=placed,
        out_specs=(P(DP, MP, None), P(MP, DP), P()),
        check_vma=False,
    )
```

profile of v0, /device:TPU:1, one launch (start us, length us, event | category | flops | bytes accessed | tf_op | source)
XLA Modules:
  0.0 240.9 jit_solution(73632805947021888)
XLA Ops:
  7.9 49.6 %all-gather.2.cloned.1.call-done = bf16[512,6144]{1,0:T(8,128)(2,1)} async-done(((bf16[512,768]{1,0:T(8,128)(2,1)}), bf16[512,6144]{1,0:T(8,128)(2,1)}) %all-gather.2.cloned.1.call-update) | async-done | bytes 6291472 | tf_op jit(solution)/shard_map/all_gather | solution.py:86
  57.5 6.9 %fusion = bf16[384,6144]{1,0:T(8,128)(2,1)S(1)} fusion(bf16[512,384]{1,0:T(8,128)(2,1)} %param.5, bf16[512,6144]{1,0:T(8,128)(2,1)} %all-gather.2.cloned.1.call-done, bf16[1,384,6144]{2,1,0:T(8,128)(2,1)} %param.7), kind=kOutput, calls=%fused_computation.1 | convolution fusion | flops 2422996992 | bytes 16121856 | tf_op jit(solution)/shard_map/dot_general | solution.py:84
  64.4 2.2 copy-done.1
  66.6 1.4 fusion.8
  68.2 18.4 %all_to_all.35 = f32[32,1,768]{2,1,0:T(1,128)S(1)} all-to-all(f32[32,1,768]{2,1,0:T(1,128)S(1)} %reshape.29), channel_id=1, replica_groups=mesh['dp_0'=8,'dp_1'=4,'mp_0'=4,'mp_1'=2] {'dp_0','dp_1'}, dimensions={0} | all-to-all | bytes 196608 | tf_op jit(solution)/shard_map/all_to_all | solution.py:19
  87.1 0.9 reduce.6
  88.3 12.3 %all_to_all.36 = f32[32,1,768]{2,1,0:T(1,128)S(1)} all-to-all(f32[32,1,768]{2,1,0:T(1,128)S(1)} %reshape.31), channel_id=1, replica_groups=mesh['dp_0'=8,'dp_1'=4,'mp_0'=4,'mp_1'=2] {'dp_0','dp_1'}, dimensions={0} | all-to-all | bytes 196608 | tf_op jit(solution)/shard_map/all_to_all | solution.py:38
  100.6 0.9 reduce.7
  102.2 0.8 reshape.33
  103.0 6.2 %all-to-all-start.2 = ((f32[8,1,4096]{2,1,0:T(1,128)}), f32[8,1,4096]{2,1,0:T(1,128)S(1)}, u32[]{:S(2)}, u32[]{:S(2)}) async-start(f32[8,1,4096]{2,1,0:T(1,128)} %reshape.33), calls=%async_computation.2 | async-start | bytes 262144 | tf_op jit(solution)/shard_map/all_to_all | solution.py:38
  109.2 5.2 %all-to-all-done.2 = f32[8,1,4096]{2,1,0:T(1,128)S(1)} async-done(((f32[8,1,4096]{2,1,0:T(1,128)}), f32[8,1,4096]{2,1,0:T(1,128)S(1)}, u32[]{:S(2)}, u32[]{:S(2)}) %all-to-all-start.2) | async-done | bytes 131104 | tf_op jit(solution)/shard_map/all_to_all | solution.py:38
  114.5 1.0 reduce.8
  115.6 5.8 %cholesky.16 = f32[64,64]{1,0:T(8,128)S(1)} custom-call(f32[64,64]{1,0:T(8,128)S(1)} %fusion.6), custom_call_target="Cholesky" | custom-call | tf_op jit(solution)/shard_map/jit(cholesky)/cholesky | solution.py:100
  122.8 4.9 %custom-call.7 = f32[1,64,64]{1,2,0:T(8,128)S(1)} custom-call(f32[1,64,64]{2,1,0:T(8,128)S(1)} %fusion.4), custom_call_target="InvertDiagBlocksLowerTriangular" | custom-call | tf_op jit(solution)/shard_map/jit(_solve_triangular)/triangular_solve | solution.py:101
  128.2 3.8 %fusion.9 = f32[6144,64]{1,0:T(8,128)S(1)} fusion(bf16[384,6144]{1,0:T(8,128)(2,1)} %copy-done.1, bf16[384,64]{0,1:T(8,128)(2,1)S(1)} %convolution_convert_fusion), kind=kOutput, calls=%fused_computation.21 | convolution fusion | flops 301989888 | bytes 6340608 | tf_op jit(solution)/shard_map/dot_general | solution.py:105
  132.0 1.9 copy.27
  133.9 3.8 %reshape.35 = f32[8,1,49152]{2,1,0:T(1,128)S(1)} reshape(f32[8,32,24,64]{3,2,1,0:T(8,128)} %copy.27) | data formatting | bytes 3145728
  137.7 24.6 %all_to_all.37 = f32[8,1,49152]{2,1,0:T(1,128)} all-to-all(f32[8,1,49152]{2,1,0:T(1,128)S(1)} %reshape.35), channel_id=1, replica_groups=mesh['dp_0'=8,'dp_1'=4,'mp_0'=4,'mp_1'=2] {'mp_0','mp_1'}, dimensions={0} | all-to-all | bytes 3145728 | tf_op jit(solution)/shard_map/all_to_all | solution.py:19
  162.2 5.8 %reduce.9 = f32[8,49152]{1,0:T(8,128)S(1)} reduce(f32[8,1,49152]{2,1,0:T(1,128)} %all_to_all.37, f32[]{:T(128)} %broadcast.54), dimensions={1}, to_apply=%all_to_all.24.reduce_sub_computation | reduce | bytes 3145732 | tf_op jit(solution)/shard_map/all_to_all | solution.py:19
  168.0 2.9 %reshape.36 = f32[8,32,24,64]{3,2,1,0:T(8,128)} reshape(f32[8,49152]{1,0:T(8,128)S(1)} %reduce.9) | data formatting | bytes 3145728
  171.0 2.1 reduce_sum.38
  173.3 13.0 %all_to_all.38 = f32[32,1,1536]{2,1,0:T(1,128)S(1)} all-to-all(f32[32,1,1536]{2,1,0:T(1,128)S(1)} %reshape.37), channel_id=1, replica_groups=mesh['dp_0'=8,'dp_1'=4,'mp_0'=4,'mp_1'=2] {'dp_0','dp_1'}, dimensions={0} | all-to-all | bytes 393216 | tf_op jit(solution)/shard_map/all_to_all | solution.py:65
  186.3 1.1 reduce.10
  187.8 12.9 %all_to_all.39 = bf16[32,2,768]{2,1,0:T(2,128)(2,1)S(1)} all-to-all(bf16[32,2,768]{2,1,0:T(2,128)(2,1)S(1)} %reshape.39), channel_id=1, replica_groups=mesh['dp_0'=8,'dp_1'=4,'mp_0'=4,'mp_1'=2] {'dp_0','dp_1'}, dimensions={0} | all-to-all | bytes 196608 | tf_op jit(solution)/shard_map/all_to_all | solution.py:38
  201.1 1.9 reshape.41
  203.0 6.9 %all-to-all-start.6 = ((bf16[8,2,24576]{2,1,0:T(2,128)(2,1)}), bf16[8,2,24576]{2,1,0:T(2,128)(2,1)S(1)}, u32[]{:S(2)}, u32[]{:S(2)}) async-start(bf16[8,2,24576]{2,1,0:T(2,128)(2,1)} %reshape.41), calls=%async_computation.6 | async-start | bytes 1572864 | tf_op jit(solution)/shard_map/all_to_all | solution.py:38
  209.9 12.2 %all-to-all-done.6 = bf16[8,2,24576]{2,1,0:T(2,128)(2,1)S(1)} async-done(((bf16[8,2,24576]{2,1,0:T(2,128)(2,1)}), bf16[8,2,24576]{2,1,0:T(2,128)(2,1)S(1)}, u32[]{:S(2)}, u32[]{:S(2)}) %all-to-all-start.6) | async-done | bytes 786464 | tf_op jit(solution)/shard_map/all_to_all | solution.py:38
  222.1 1.9 reshape.42
  224.0 1.8 copy.28
  225.8 6.0 %fusion.1 = bf16[1,384,6144]{2,1,0:T(8,128)(2,1)} fusion(bf16[384,64]{0,1:T(8,128)(2,1)S(1)} %convolution_convert_fusion, bf16[6144,64]{1,0:T(8,128)(2,1)S(1)} %bitcast.33, bf16[384,6144]{1,0:T(8,128)(2,1)} %copy-done.1), kind=kOutput, calls=%fused_computation.3 | convolution fusion | flops 311427072 | bytes 10272768 | tf_op jit(solution)/shard_map/dot_general | solution.py:114
  231.8 1.4 copy.29
  233.2 0.9 convolution_add_fusion
  (33 shorter events, 5.3 us)
Async XLA Ops:
  7.2 59.5 %copy-start = (bf16[6144,64]{0,1:T(8,128)(2,1)S(1)}, bf16[6144,64]{0,1:T(8,128)(2,1)}, u32[]{:S(2)}) copy-start(bf16[6144,64]{0,1:T(8,128)(2,1)} %param.8) | copy-start | bytes 2359300
  7.2 50.3 %all-gather.2.cloned.1.call-start = ((), (), s32[]{:S(2)}) async-start(), calls=%async_computation.7 | async-start | bytes 7077888 | tf_op jit(solution)/shard_map/all_gather | solution.py:86
  64.4 2.2 copy-start.1
  103.0 11.5 %all-to-all-start.2 = ((f32[8,1,4096]{2,1,0:T(1,128)}), f32[8,1,4096]{2,1,0:T(1,128)S(1)}, u32[]{:S(2)}, u32[]{:S(2)}) async-start(f32[8,1,4096]{2,1,0:T(1,128)} %reshape.33), calls=%async_computation.2 | async-start | bytes 262144 | tf_op jit(solution)/shard_map/all_to_all | solution.py:38
  203.0 19.1 %all-to-all-start.6 = ((bf16[8,2,24576]{2,1,0:T(2,128)(2,1)}), bf16[8,2,24576]{2,1,0:T(2,128)(2,1)S(1)}, u32[]{:S(2)}, u32[]{:S(2)}) async-start(bf16[8,2,24576]{2,1,0:T(2,128)(2,1)} %reshape.41), calls=%async_computation.6 | async-start | bytes 1572864 | tf_op jit(solution)/shard_map/all_to_all | solution.py:38
  225.8 7.4 %copy-start.2 = (f32[384,192]{0,1:T(8,128)S(1)}, f32[384,192]{0,1:T(8,128)}, u32[]{:S(2)}) copy-start(f32[384,192]{0,1:T(8,128)} %param.9) | copy-start | bytes 884740
Sparse Core Ops, SparseCore 0:
  9.8 47.6 all-gather.1
where the time goes:
time: 242 us; the launch traced here: 241 us
  blocking collectives  81.1 us (34%)
  waiting for transfers between devices  67.7 us (28%)
  other arithmetic  23.9 us (10%)
  local copies, waits for them, and re-layouts  20.9 us (9%)
  matrix products  20 us (8%)
  between operations  14.3 us (6%)
  starting transfers between devices  13.1 us (5%)
    all_gather x1, waiting for transfers between devices, local(): lax.all_gather(out_grads, MP, axis=1, tiled=True)  49.6 us
    all_to_all x2, blocking collectives, summed_on_arrival(): lax.all_to_all(blocks, axis, split_axis=0, concat_axis=0, tiled=True)  43 us
    all_to_all x2, blocking collectives, copy_for_each(): return lax.all_to_all(copies, axis, split_axis=0, concat_axis=0, tiled=True)  25.2 us
    all_to_all x2, waiting for transfers between devices, copy_for_each(): return lax.all_to_all(copies, axis, split_axis=0, concat_axis=0, tiled=True)  17.4 us
    unnamed x21, local copies, waits for them, and re-layouts  16.3 us
    all_to_all x2, starting transfers between devices, copy_for_each(): return lax.all_to_all(copies, axis, split_axis=0, concat_axis=0, tiled=True)  13.1 us
    all_to_all x1, blocking collectives, sum_in_two_steps(): return jnp.sum(lax.all_to_all(own, far, 0, 0, tiled=True), axis=0)  13 us
    dot_general x1, matrix products, local(): lax.dot_general(activations, lax.all_gather(out_grads, MP, axis=1, tiled=...  6.95 us
  transfers between devices with their start and end apart: 3, of which 3 were waited for; matrix products, arithmetic and copies ran while one was open for 0% of the time, Pallas kernels for 0%

commit v1 on v0

--- a/solution.py
+++ b/solution.py
@@ -83,7 +83,9 @@
     own_error = error[0]
     product = lax.dot_general(
         activations,
-        lax.all_gather(out_grads, MP, axis=1, tiled=True),
+        jnp.concatenate(
+            lax.all_to_all(jnp.stack([out_grads] * lax.axis_size(MP)), MP, 0, 0), axis=1
+        ),
         (((0,), (0,)), ((), ())),
         preferred_element_type=jnp.float32,
     )

time: 242 us -> 255 us (1.054)
  blocking collectives: 81.1 us -> 160 us
  waiting for transfers between devices: 67.7 us -> 17.4 us
  between operations: 14.3 us -> 0.92 us
  matrix products: 20 us -> 15.9 us
    all_to_all x0 -> x1, blocking collectives: none -> 77.1 us  [local(): lax.all_to_all(jnp.stack([out_grads] * lax.axis_size(MP)), MP, 0, 0)]
    all_gather x1 -> x0, waiting for transfers between devices: 49.6 us -> none  [local(): lax.all_gather(out_grads, MP, axis=1, tiled=True)]
    dot_general x1, matrix products: 6.95 us -> 2.91 us  [local(): lax.dot_general(activations, jnp.concatenate(lax.all_to_all(jnp.stack([ou...]
    unnamed x21 -> x28, local copies, waits for them, and re-layouts: 16.3 us -> 17.8 us
  transfers between devices with their start and end apart: 3 -> 2, of which waited for: 3 -> 2; matrix products, arithmetic and copies ran while one was open for 0% -> 0% of each run, Pallas kernels for 0% -> 0%
where the time goes in v1:
time: 255 us
  blocking collectives  160 us (63%)
  other arithmetic  23.9 us (9%)
  local copies, waits for them, and re-layouts  22.9 us (9%)
  waiting for transfers between devices  17.4 us (7%)
  matrix products  15.9 us (6%)
  starting transfers between devices  13.8 us (5%)
    all_to_all x1, blocking collectives, local(): lax.all_to_all(jnp.stack([out_grads] * lax.axis_size(MP)), MP, 0, 0)  77.1 us
    all_to_all x2, blocking collectives, summed_on_arrival(): lax.all_to_all(blocks, axis, split_axis=0, concat_axis=0, tiled=True)  44.5 us
    all_to_all x2, blocking collectives, copy_for_each(): return lax.all_to_all(copies, axis, split_axis=0, concat_axis=0, tiled=True)  25.2 us
    unnamed x28, local copies, waits for them, and re-layouts  17.8 us
    all_to_all x2, waiting for transfers between devices, copy_for_each(): return lax.all_to_all(copies, axis, split_axis=0, concat_axis=0, tiled=True)  17.4 us
    all_to_all x2, starting transfers between devices, copy_for_each(): return lax.all_to_all(copies, axis, split_axis=0, concat_axis=0, tiled=True)  13.8 us
    all_to_all x1, blocking collectives, sum_in_two_steps(): return jnp.sum(lax.all_to_all(own, far, 0, 0, tiled=True), axis=0)  13 us
    all_to_all x2, other arithmetic, summed_on_arrival(): lax.all_to_all(blocks, axis, split_axis=0, concat_axis=0, tiled=True)  6.67 us
  transfers between devices with their start and end apart: 2, of which 2 were waited for; matrix products, arithmetic and copies ran while one was open for 0% of the time, Pallas kernels for 0%

profile of v1, /device:TPU:1, one launch (start us, length us, event | category | flops | bytes accessed | tf_op | source)
XLA Modules:
  0.0 254.7 jit_solution(904935183737858082)
XLA Ops:
  0.6 1.5 copy.24
  2.7 77.1 %all_to_all.40 = bf16[8,512,768]{1,2,0:T(8,128)(2,1)S(1)} all-to-all(bf16[8,512,768]{1,2,0:T(8,128)(2,1)S(1)} %stack.2), channel_id=1, replica_groups=mesh['dp_0'=8,'dp_1'=4,'mp_0'=4,'mp_1'=2] {'mp_0','mp_1'}, dimensions={0} | all-to-all | bytes 12582912 | tf_op jit(solution)/shard_map/all_to_all | solution.py:87
  79.9 2.9 %fusion = bf16[384,6144]{1,0:T(8,128)(2,1)S(1)} fusion(bf16[512,384]{1,0:T(8,128)(2,1)S(1)} %copy-done.3, bf16[512,6144]{0,1:T(8,128)(2,1)S(1)} %bitcast.40, bf16[1,384,6144]{2,1,0:T(8,128)(2,1)S(1)} %bitcast.43), kind=kOutput, calls=%fused_computation.1 | convolution fusion | flops 2422996992 | bytes 16121856 | tf_op jit(solution)/shard_map/dot_general | solution.py:84
  82.8 2.2 copy-done.1
  85.0 1.4 fusion.8
  86.5 19.9 %all_to_all.41 = f32[32,1,768]{2,1,0:T(1,128)S(1)} all-to-all(f32[32,1,768]{2,1,0:T(1,128)S(1)} %reshape.39), channel_id=1, replica_groups=mesh['dp_0'=8,'dp_1'=4,'mp_0'=4,'mp_1'=2] {'dp_0','dp_1'}, dimensions={0} | all-to-all | bytes 196608 | tf_op jit(solution)/shard_map/all_to_all | solution.py:19
  107.0 0.9 reduce.6
  108.2 12.3 %all_to_all.42 = f32[32,1,768]{2,1,0:T(1,128)S(1)} all-to-all(f32[32,1,768]{2,1,0:T(1,128)S(1)} %reshape.41), channel_id=1, replica_groups=mesh['dp_0'=8,'dp_1'=4,'mp_0'=4,'mp_1'=2] {'dp_0','dp_1'}, dimensions={0} | all-to-all | bytes 196608 | tf_op jit(solution)/shard_map/all_to_all | solution.py:38
  120.5 0.9 reduce.7
  122.8 6.9 %all-to-all-start.3 = ((f32[8,1,4096]{2,1,0:T(1,128)}), f32[8,1,4096]{2,1,0:T(1,128)S(1)}, u32[]{:S(2)}, u32[]{:S(2)}) async-start(f32[8,1,4096]{2,1,0:T(1,128)} %reshape.43), calls=%async_computation.3 | async-start | bytes 262144 | tf_op jit(solution)/shard_map/all_to_all | solution.py:38
  129.8 5.2 %all-to-all-done.3 = f32[8,1,4096]{2,1,0:T(1,128)S(1)} async-done(((f32[8,1,4096]{2,1,0:T(1,128)}), f32[8,1,4096]{2,1,0:T(1,128)S(1)}, u32[]{:S(2)}, u32[]{:S(2)}) %all-to-all-start.3) | async-done | bytes 131104 | tf_op jit(solution)/shard_map/all_to_all | solution.py:38
  135.0 1.0 reduce.8
  136.2 5.8 %cholesky.16 = f32[64,64]{1,0:T(8,128)S(1)} custom-call(f32[64,64]{1,0:T(8,128)S(1)} %fusion.6), custom_call_target="Cholesky" | custom-call | tf_op jit(solution)/shard_map/jit(cholesky)/cholesky | solution.py:102
  143.4 4.9 %custom-call.7 = f32[1,64,64]{1,2,0:T(8,128)S(1)} custom-call(f32[1,64,64]{2,1,0:T(8,128)S(1)} %fusion.4), custom_call_target="InvertDiagBlocksLowerTriangular" | custom-call | tf_op jit(solution)/shard_map/jit(_solve_triangular)/triangular_solve | solution.py:103
  148.7 3.8 %fusion.9 = f32[6144,64]{1,0:T(8,128)S(1)} fusion(bf16[384,6144]{1,0:T(8,128)(2,1)} %copy-done.1, bf16[384,64]{0,1:T(8,128)(2,1)S(1)} %convolution_convert_fusion), kind=kOutput, calls=%fused_computation.21 | convolution fusion | flops 301989888 | bytes 6340608 | tf_op jit(solution)/shard_map/dot_general | solution.py:107
  152.6 1.9 copy.30
  154.4 3.8 %reshape.45 = f32[8,1,49152]{2,1,0:T(1,128)S(1)} reshape(f32[8,32,24,64]{3,2,1,0:T(8,128)} %copy.30) | data formatting | bytes 3145728
  158.3 24.6 %all_to_all.43 = f32[8,1,49152]{2,1,0:T(1,128)} all-to-all(f32[8,1,49152]{2,1,0:T(1,128)S(1)} %reshape.45), channel_id=1, replica_groups=mesh['dp_0'=8,'dp_1'=4,'mp_0'=4,'mp_1'=2] {'mp_0','mp_1'}, dimensions={0} | all-to-all | bytes 3145728 | tf_op jit(solution)/shard_map/all_to_all | solution.py:19
  182.8 5.8 %reduce.9 = f32[8,49152]{1,0:T(8,128)S(1)} reduce(f32[8,1,49152]{2,1,0:T(1,128)} %all_to_all.43, f32[]{:T(128)} %broadcast.56), dimensions={1}, to_apply=%all_to_all.28.reduce_sub_computation | reduce | bytes 3145732 | tf_op jit(solution)/shard_map/all_to_all | solution.py:19
  188.6 2.9 %reshape.46 = f32[8,32,24,64]{3,2,1,0:T(8,128)} reshape(f32[8,49152]{1,0:T(8,128)S(1)} %reduce.9) | data formatting | bytes 3145728
  191.5 2.1 reduce_sum.38
  193.9 13.0 %all_to_all.44 = f32[32,1,1536]{2,1,0:T(1,128)S(1)} all-to-all(f32[32,1,1536]{2,1,0:T(1,128)S(1)} %reshape.47), channel_id=1, replica_groups=mesh['dp_0'=8,'dp_1'=4,'mp_0'=4,'mp_1'=2] {'dp_0','dp_1'}, dimensions={0} | all-to-all | bytes 393216 | tf_op jit(solution)/shard_map/all_to_all | solution.py:65
  206.9 1.1 reduce.10
  208.3 12.9 %all_to_all.45 = bf16[32,2,768]{2,1,0:T(2,128)(2,1)S(1)} all-to-all(bf16[32,2,768]{2,1,0:T(2,128)(2,1)S(1)} %reshape.49), channel_id=1, replica_groups=mesh['dp_0'=8,'dp_1'=4,'mp_0'=4,'mp_1'=2] {'dp_0','dp_1'}, dimensions={0} | all-to-all | bytes 196608 | tf_op jit(solution)/shard_map/all_to_all | solution.py:38
  221.7 1.9 reshape.51
  223.6 6.9 %all-to-all-start.7 = ((bf16[8,2,24576]{2,1,0:T(2,128)(2,1)}), bf16[8,2,24576]{2,1,0:T(2,128)(2,1)S(1)}, u32[]{:S(2)}, u32[]{:S(2)}) async-start(bf16[8,2,24576]{2,1,0:T(2,128)(2,1)} %reshape.51), calls=%async_computation.7 | async-start | bytes 1572864 | tf_op jit(solution)/shard_map/all_to_all | solution.py:38
  230.4 12.2 %all-to-all-done.7 = bf16[8,2,24576]{2,1,0:T(2,128)(2,1)S(1)} async-done(((bf16[8,2,24576]{2,1,0:T(2,128)(2,1)}), bf16[8,2,24576]{2,1,0:T(2,128)(2,1)S(1)}, u32[]{:S(2)}, u32[]{:S(2)}) %all-to-all-start.7) | async-done | bytes 786464 | tf_op jit(solution)/shard_map/all_to_all | solution.py:38
  242.6 1.9 reshape.52
  244.5 1.8 copy.31
  246.4 6.0 %fusion.1 = bf16[1,384,6144]{2,1,0:T(8,128)(2,1)} fusion(bf16[384,64]{0,1:T(8,128)(2,1)S(1)} %convolution_convert_fusion, bf16[6144,64]{1,0:T(8,128)(2,1)S(1)} %bitcast.36, bf16[384,6144]{1,0:T(8,128)(2,1)} %copy-done.1), kind=kOutput, calls=%fused_computation.3 | convolution fusion | flops 311427072 | bytes 10272768 | tf_op jit(solution)/shard_map/dot_general | solution.py:116
  252.4 1.4 copy.32
  253.8 0.9 convolution_add_fusion
  (40 shorter events, 6.0 us)
Async XLA Ops:
  0.6 84.3 %copy-start = (bf16[6144,64]{0,1:T(8,128)(2,1)S(1)}, bf16[6144,64]{0,1:T(8,128)(2,1)}, u32[]{:S(2)}) copy-start(bf16[6144,64]{0,1:T(8,128)(2,1)} %param.8) | copy-start | bytes 2359300
  2.1 77.7 %slice-start = ((s8[4718592]{0:T(1024)(128)(4,1)}), s8[524288]{0:T(1024)(128)(4,1)S(1)}, s32[]{:S(2)}) async-start(s8[4718592]{0:T(1024)(128)(4,1)} %bitcast.42), calls=%async_computation.8 | async-start | bytes 1048576
  2.7 77.2 %slice-start.1 = ((s8[4718592]{0:T(1024)(128)(4,1)}), s8[4194304]{0:T(1024)(128)(4,1)S(1)}, s32[]{:S(2)}) async-start(s8[4718592]{0:T(1024)(128)(4,1)} %bitcast.42), calls=%async_computation.9 | async-start | bytes 8388608
  2.7 77.2 %copy-start.3 = (bf16[512,384]{1,0:T(8,128)(2,1)S(1)}, bf16[512,384]{1,0:T(8,128)(2,1)}, u32[]{:S(2)}) copy-start(bf16[512,384]{1,0:T(8,128)(2,1)} %param.5) | copy-start | bytes 1179652
  82.8 2.2 copy-start.1
  122.8 12.2 %all-to-all-start.3 = ((f32[8,1,4096]{2,1,0:T(1,128)}), f32[8,1,4096]{2,1,0:T(1,128)S(1)}, u32[]{:S(2)}, u32[]{:S(2)}) async-start(f32[8,1,4096]{2,1,0:T(1,128)} %reshape.43), calls=%async_computation.3 | async-start | bytes 262144 | tf_op jit(solution)/shard_map/all_to_all | solution.py:38
  223.6 19.1 %all-to-all-start.7 = ((bf16[8,2,24576]{2,1,0:T(2,128)(2,1)}), bf16[8,2,24576]{2,1,0:T(2,128)(2,1)S(1)}, u32[]{:S(2)}, u32[]{:S(2)}) async-start(bf16[8,2,24576]{2,1,0:T(2,128)(2,1)} %reshape.51), calls=%async_computation.7 | async-start | bytes 1572864 | tf_op jit(solution)/shard_map/all_to_all | solution.py:38
  246.4 7.4 %copy-start.2 = (f32[384,192]{0,1:T(8,128)S(1)}, f32[384,192]{0,1:T(8,128)}, u32[]{:S(2)}) copy-start(f32[384,192]{0,1:T(8,128)} %param.9) | copy-start | bytes 884740
